TPU v7x, 32 devices: a whole 2x2x4 slice. The times are simulated.
32 devices in a mesh: dp: 2 (over x), row: 4 (over y, core), col: 4 (over z).
Axes of the slice: x: 2, y: 2, z: 4, core: 2. Of those that a mesh axis runs over, the one named last changes fastest.
Arguments:
- latents: float32 [24, 32, 128], P(('dp', 'row')), may hold values from -6 to 6
- labels: int32 [24], P(('dp', 'row')), may hold values from 0 to 999
- step_index: int32 [24], P(('dp', 'row')), may hold values from 1 to 8
- seeds: int32 [24], P(('dp', 'row')), may hold values from 0 to 2147483646
- class_table: bfloat16 [1000, 1152], replicated, may hold values from -6 to 6
- teacher_patch: bfloat16 [16, 1152], replicated, may hold values from -1.5 to 1.5
- teacher_mod: bfloat16 [1152, 3, 1152], P(('dp', 'row'), None, 'col'), may hold values from -0.1875 to 0.1875
- teacher_up: bfloat16 [1152, 4608], P(('dp', 'row'), 'col'), may hold values from -0.1875 to 0.1875
- teacher_down: bfloat16 [1152, 4608], P(('dp', 'row'), 'col'), may hold values from -0.09375 to 0.09375
- teacher_out: bfloat16 [16, 1152], replicated, may hold values from -0.1875 to 0.1875
- student_patch: bfloat16 [16, 1152], replicated, may hold values from -1.5 to 1.5
- student_mod: bfloat16 [1152, 3, 1152], P(('dp', 'row'), None, 'col'), may hold values from -0.1875 to 0.1875
- student_up: bfloat16 [1152, 4608], P(('dp', 'row'), 'col'), may hold values from -0.1875 to 0.1875
- student_down: bfloat16 [1152, 4608], P(('dp', 'row'), 'col'), may hold values from -0.09375 to 0.09375
- student_out: bfloat16 [16, 1152], replicated, may hold values from -0.1875 to 0.1875
Outputs:
- up_gradient: float32 [1152, 4608], P(('dp', 'row'), 'col')
- down_gradient: float32 [1152, 4608], P(('dp', 'row'), 'col')
All inputs are finite; a program needn't handle non-finite values.
Results may differ from a plain program's by a relative error of at most 0.002.
Values may be sent and summed in bfloat16 or wider, within the bound.
No kernel may reach another device: no remote copies, remote signals or barrier semaphores. Data moves between devices by JAX's collectives and lax.ppermute only.
A program may use at most 128 MiB of HBM per device.

v0:
```python
import math
import jax
import jax.numpy as jnp
from jax import lax
from jax.sharding import PartitionSpec as P

D = 1152
CLASSES = 1000
SEQ = 256
PATCH = 16
STEPS = 8
HALF_PI = 0.5 * math.pi
ROOT_TWO_PI = math.sqrt(2.0 / math.pi)


def plan(times):
    return (jnp.cos(HALF_PI * times), jnp.sin(HALF_PI * times))


def mixing(value):
    amount = jnp.int32(16)
    value = value ^ lax.shift_right_logical(value, amount)
    value = value * 73244475
    value = value ^ lax.shift_right_logical(value, amount)
    value = value * 73244475
    value = value ^ lax.shift_right_logical(value, amount)
    return value


def noise_of(seeds):
    total = SEQ * PATCH
    places = jnp.arange(total, dtype=jnp.int32).reshape(1, total // 128, 128)
    mixed = mixing(seeds[:, None, None] * 1103515245 + places * 40503 + 12345)
    uniform = (lax.shift_right_logical(mixed, jnp.int32(8)).astype(jnp.float32) + 0.5) * (
        1.0 / 16777216.0
    )
    return math.sqrt(2.0) * lax.erf_inv(2.0 * uniform - 1.0)


def time_features(times):
    half = D // 2
    freqs = jnp.exp(-math.log(10000.0) * jnp.arange(half, dtype=jnp.float32) / half)
    angle = (1000.0 * times)[:, None] * freqs[None, :]
    return jnp.concatenate([jnp.cos(angle), jnp.sin(angle)], axis=1)


def condition(times, labels, class_table):
    onehot = (labels[:, None] == jnp.arange(CLASSES, dtype=jnp.int32)[None, :]).astype(jnp.bfloat16)
    embedded = jnp.dot(onehot, class_table, preferred_element_type=jnp.float32)
    return jax.nn.silu(embedded + time_features(times)).astype(jnp.bfloat16)


def positions():
    quarter = D // 4
    omega = 1.0 / 10000.0 ** (jnp.arange(quarter, dtype=jnp.float32) / quarter)
    side = math.isqrt(SEQ)
    cells = jnp.arange(SEQ, dtype=jnp.int32)
    grid_row = (cells // side).astype(jnp.float32)
    grid_col = (cells % side).astype(jnp.float32)
    row_angle = grid_row[:, None] * omega[None, :]
    col_angle = grid_col[:, None] * omega[None, :]
    return jnp.concatenate(
        [jnp.sin(row_angle), jnp.cos(row_angle), jnp.sin(col_angle), jnp.cos(col_angle)], axis=1
    )


def layer_norm(values):
    center = values - jnp.mean(values, axis=-1, keepdims=True)
    spread = jnp.mean(center * center, axis=-1, keepdims=True)
    reciprocal = lax.rsqrt(spread + 1e-06)
    return (center * reciprocal, reciprocal)


def gelu_slope(pre):
    inner = ROOT_TWO_PI * (pre + 0.044715 * pre * pre * pre)
    tangent = jnp.tanh(inner)
    return 0.5 * (1.0 + tangent) + 0.5 * pre * (1.0 - tangent * tangent) * ROOT_TWO_PI * (
        1.0 + 3.0 * 0.044715 * pre * pre
    )


def contract_last(left, right):
    return lax.dot_general(
        left, right, (((1,), (1,)), ((), ())), preferred_element_type=jnp.float32
    )


def contract_first(left, right):
    return lax.dot_general(
        left, right, (((0,), (0,)), ((), ())), preferred_element_type=jnp.float32
    )


def network(state, mods, patch_weight, out_weight, pos, up_product, down_product):
    samples = state.shape[0]
    tokens = state.reshape(samples * SEQ, PATCH).astype(jnp.bfloat16)
    base = (
        jnp.dot(tokens, patch_weight, preferred_element_type=jnp.float32).reshape(samples, SEQ, D)
        + pos[None]
    )
    shift = mods[:, 0][:, None, :]
    scale = mods[:, 1][:, None, :]
    gate = mods[:, 2][:, None, :]
    normed, _ = layer_norm(base)
    act = (normed * (1.0 + scale) + shift).astype(jnp.bfloat16).reshape(samples * SEQ, D)
    pre = up_product(act)
    hidden = jax.nn.gelu(pre, approximate=True).astype(jnp.bfloat16)
    partial_out = down_product(hidden).astype(jnp.bfloat16)
    mixed = lax.psum(partial_out, "col").astype(jnp.float32)
    later = base + gate * mixed.reshape(samples, SEQ, D)
    final, reciprocal = layer_norm(later)
    velocity = contract_last(final.astype(jnp.bfloat16).reshape(samples * SEQ, D), out_weight)
    return (
        velocity.reshape(samples, SEQ * PATCH // 128, 128),
        (act, pre, hidden, final, reciprocal, gate, out_weight),
    )


def reduce_gradient(left, right):
    return lax.psum_scatter(
        contract_first(left, right), ("dp", "row"), scatter_dimension=0, tiled=True
    )


def body(
    latents,
    labels,
    step_index,
    seeds,
    class_table,
    teacher_patch,
    teacher_mod,
    teacher_up,
    teacher_down,
    teacher_out,
    student_patch,
    student_mod,
    student_up,
    student_down,
    student_out,
):
    samples = latents.shape[0]
    batch_total = samples * lax.axis_size(("dp", "row"))
    pos = positions()
    all_labels, all_steps = (
        lax.all_gather(labels, ("dp", "row"), axis=0, tiled=True),
        lax.all_gather(step_index, ("dp", "row"), axis=0, tiled=True),
    )
    all_now = all_steps.astype(jnp.float32) / STEPS
    cond_now = condition(all_now, all_labels, class_table)
    cond_mid = condition(all_now - 0.5 / STEPS, all_labels, class_table)
    own_rows = teacher_mod.shape[0]
    offset = lax.axis_index(("dp", "row")) * own_rows
    rows_now = lax.dynamic_slice_in_dim(cond_now, offset, own_rows, 1)
    rows_mid = lax.dynamic_slice_in_dim(cond_mid, offset, own_rows, 1)
    teacher_part = jnp.einsum(
        "nkd,dcf->nkcf",
        jnp.stack([rows_now, rows_mid], axis=1),
        teacher_mod,
        preferred_element_type=jnp.float32,
    )
    student_part = jnp.einsum(
        "nd,dcf->ncf", rows_now, student_mod, preferred_element_type=jnp.float32
    )[:, None]
    teacher_sums, student_sums = (
        lax.psum_scatter(teacher_part, ("dp", "row"), scatter_dimension=0, tiled=True),
        lax.psum_scatter(student_part, ("dp", "row"), scatter_dimension=0, tiled=True),
    )
    teacher_mods, student_mods = (
        lax.all_gather(teacher_sums, "col", axis=3, tiled=True),
        lax.all_gather(student_sums, "col", axis=3, tiled=True),
    )
    now = step_index.astype(jnp.float32) / STEPS
    alpha, sigma = plan(now[:, None, None])
    alpha_mid, sigma_mid = plan((now - 0.5 / STEPS)[:, None, None])
    alpha_end, sigma_end = plan((now - 1.0 / STEPS)[:, None, None])
    noisy = alpha * latents + sigma * noise_of(seeds)
    up_panel, down_panel = (
        lax.all_gather(teacher_up, ("dp", "row"), axis=0, tiled=True),
        lax.all_gather(teacher_down, ("dp", "row"), axis=0, tiled=True),
    )

    def teacher_up_product(act):
        return jnp.dot(act, up_panel, preferred_element_type=jnp.float32)

    def teacher_down_product(hidden):
        return contract_last(hidden, down_panel)

    first_v, _ = network(
        noisy,
        teacher_mods[:, 0],
        teacher_patch,
        teacher_out,
        pos,
        teacher_up_product,
        teacher_down_product,
    )
    first_x = alpha * noisy - sigma * first_v
    halfway = alpha_mid * first_x + sigma_mid * (noisy - alpha * first_x) / sigma
    second_v, _ = network(
        halfway,
        teacher_mods[:, 1],
        teacher_patch,
        teacher_out,
        pos,
        teacher_up_product,
        teacher_down_product,
    )
    second_x = alpha_mid * halfway - sigma_mid * second_v
    landing = alpha_end * second_x + sigma_end * (halfway - alpha_mid * second_x) / sigma_mid
    ratio = sigma_end / sigma
    target = (landing - ratio * noisy) / (alpha_end - ratio * alpha)

    def student_up_product(act):
        return jnp.dot(
            act,
            lax.all_gather(student_up, ("dp", "row"), axis=0, tiled=True),
            preferred_element_type=jnp.float32,
        )

    student_panel = lax.all_gather(student_down, ("dp", "row"), axis=0, tiled=True)

    def student_down_product(hidden):
        return contract_last(hidden, student_panel)

    student_v, saved = network(
        noisy,
        student_mods[:, 0],
        student_patch,
        student_out,
        pos,
        student_up_product,
        student_down_product,
    )
    student_x = alpha * noisy - sigma * student_v
    weight = jnp.maximum(alpha * alpha / (sigma * sigma), 1.0)
    back_velocity = (-2.0 * sigma * weight * (student_x - target) / batch_total).reshape(
        samples * SEQ, PATCH
    )
    act, pre, hidden, final, reciprocal, gate_share, out_share = saved
    back_final = jnp.dot(
        back_velocity, out_share.astype(jnp.float32), precision=lax.Precision.HIGHEST
    ).reshape(samples, SEQ, -1)
    centre = jnp.mean(back_final, axis=2, keepdims=True)
    along = jnp.mean(back_final * final, axis=2, keepdims=True)
    back_mixed = (
        (gate_share * (reciprocal * (back_final - centre - final * along)))
        .astype(jnp.bfloat16)
        .reshape(samples * SEQ, D)
    )
    down_gradient = reduce_gradient(back_mixed, hidden)
    back_hidden = jnp.dot(back_mixed, student_panel, preferred_element_type=jnp.float32)
    back_pre = (back_hidden * gelu_slope(pre)).astype(jnp.bfloat16)
    up_gradient = reduce_gradient(act, back_pre)
    return (up_gradient, down_gradient)


def solution(mesh):
    placed = (
        P(("dp", "row"), None, None),
        P(("dp", "row")),
        P(("dp", "row")),
        P(("dp", "row")),
        P(),
        P(),
        P(("dp", "row"), None, "col"),
        P(("dp", "row"), "col"),
        P(("dp", "row"), "col"),
        P(),
        P(),
        P(("dp", "row"), None, "col"),
        P(("dp", "row"), "col"),
        P(("dp", "row"), "col"),
        P(),
    )
    return jax.shard_map(
        body,
        mesh=mesh,
        in_specs=placed,
        out_specs=(P(("dp", "row"), "col"), P(("dp", "row"), "col")),
        check_vma=False,
    )
```

profile of v0, /device:TPU:0, one launch (start us, length us, event | category | flops | bytes accessed | tf_op | source)
XLA Modules:
  0.0 598.2 jit_solution(1822111172915230698)
XLA Ops:
  11.2 9.5 %all-reduce.4 = (s32[24]{0:T(128)S(1)}, s32[24]{0:T(128)S(1)}) all-reduce(s32[24]{0:T(128)S(1)} %dynamic-update-slice, s32[24]{0:T(128)S(1)} %dynamic-update-slice.1), channel_id=1, replica_groups=mesh['dp'=2,'row'=4,'col'=4] {'dp','row'}, use_global_device_ids=true, to_apply=%add | all-reduce | flops 48 | bytes 384
  30.0 2.8 multiply_cosine_fusion
  40.5 2.5 multiply_reduce_fusion.6
  44.3 33.5 %all-reduce.13.cloned.1.call-done = (f32[24,1,3,288]{3,1,2,0:T(1,128)}, f32[24,2,3,288]{3,1,2,0:T(2,128)}) async-done(((f32[24,1,3,288]{3,1,2,0:T(1,128)}, f32[24,2,3,288]{3,1,2,0:T(2,128)}), (f32[24,1,3,288]{3,1,2,0:T(1,128)}, f32[24,2,3,288]{3,1,2,0:T(2,128)})) %all-reduce.13.cloned.1.call-update) | async-done | bytes 248848
  81.2 62.1 %all_gather.29 = f32[3,2,3,1152]{2,1,0,3:T(2,128)S(1)} all-gather(f32[3,2,3,288]{2,1,0,3:T(2,128)} %copy.57), channel_id=1, replica_groups=mesh['dp'=2,'row'=4,'col'=4] {'col'}, dimensions={3}, use_global_device_ids=true | all-gather | bytes 103680 | tf_op jit(solution)/shard_map/all_gather | solution.py:170
  143.3 3.9 fusion.94
  147.1 4.6 copy.81
  151.7 4.6 copy.82
  158.0 38.8 %all_gather.26 = f32[3,1,3,1152]{2,1,0,3:T(1,128)} all-gather(f32[3,1,3,288]{2,1,0,3:T(1,128)} %copy.52), channel_id=1, replica_groups=mesh['dp'=2,'row'=4,'col'=4] {'col'}, dimensions={3}, use_global_device_ids=true | all-gather | bytes 51840 | tf_op jit(solution)/shard_map/all_gather | solution.py:171
  196.9 4.6 copy.53
  204.0 3.1 add_convert_fusion.1
  207.2 4.5 add_convert_fusion.2
  211.7 9.5 %convolution_convert_fusion.1 = bf16[768,1152]{1,0:T(8,128)(2,1)} fusion(bf16[1152,1152]{1,0:T(8,128)(2,1)} %all-gather.11.cloned.1.call-done, bf16[768,1152]{1,0:T(8,128)(2,1)} %bitcast.116, bf16[1152,1152]{1,0:T(8,128)(2,1)} %all-gather.9.cloned.1.call-done), kind=kOutput, calls=%fused_computation.56 | convolution fusion | flops 4085710848 | bytes 8847360 | tf_op jit(solution)/shard_map/dot_general | solution.py:83
  225.0 6.7 %fusion.106 = f32[768,1152]{1,0:T(8,128)} fusion(bf16[768,1152]{1,0:T(8,128)(2,1)} %bitcast.109, bf16[1152,1152]{1,0:T(8,128)(2,1)} %all-gather.5.cloned.1.call-done), kind=kOutput, calls=%fused_computation.198 | convolution fusion | flops 2038431744 | bytes 7962624 | tf_op jit(solution)/shard_map/dot_general | solution.py:215
  231.7 7.3 %convolution_convert_fusion.2 = bf16[768,1152]{1,0:T(8,128)(2,1)} fusion(bf16[1152,1152]{1,0:T(8,128)(2,1)} %all-gather.7.cloned.1.call-done, f32[768,1152]{1,0:T(8,128)} %fusion.106), kind=kOutput, calls=%fused_computation.57 | convolution fusion | flops 2047279104 | bytes 7962624 | tf_op jit(solution)/shard_map/dot_general | solution.py:83
  238.9 54.8 %all-reduce.11.cloned.1.call-done = bf16[3,256,1152]{2,1,0:T(8,128)(2,1)} async-done(((bf16[3,256,1152]{2,1,0:T(8,128)(2,1)}), bf16[3,256,1152]{2,1,0:T(8,128)(2,1)}) %all-reduce.11.cloned.1.call-update) | async-done | bytes 1769488 | tf_op jit(solution)/shard_map/psum | solution.py:109
  305.2 9.7 %convolution_convert_fusion = bf16[768,1152]{1,0:T(8,128)(2,1)} fusion(bf16[1152,1152]{1,0:T(8,128)(2,1)} %all-gather.11.cloned.1.call-done, bf16[768,1152]{1,0:T(8,128)(2,1)} %bitcast.117, bf16[1152,1152]{1,0:T(8,128)(2,1)} %all-gather.9.cloned.1.call-done), kind=kOutput, calls=%fused_computation.55 | convolution fusion | flops 4085710848 | bytes 8847360 | tf_op jit(solution)/shard_map/dot_general | solution.py:83
  316.9 131.0 %all-reduce.15.cloned.1.call-done = (bf16[3,256,1152]{2,1,0:T(8,128)(2,1)}, bf16[3,256,1152]{2,1,0:T(8,128)(2,1)}) async-done(((bf16[3,256,1152]{2,1,0:T(8,128)(2,1)}, bf16[3,256,1152]{2,1,0:T(8,128)(2,1)}), (bf16[3,256,1152]{2,1,0:T(8,128)(2,1)}, bf16[3,256,1152]{2,1,0:T(8,128)(2,1)})) %all-reduce.15.cloned.1.call-update) | async-done | bytes 3538960 | tf_op jit(solution)/shard_map/psum | solution.py:109
  447.9 3.1 fusion.92
  462.0 4.6 fusion.90
  469.2 5.0 fusion.87
  474.6 12.3 %fusion.110 = f32[1152,1152]{1,0:T(8,128)} fusion(bf16[768,1152]{1,0:T(8,128)(2,1)} %bitcast.110, f32[768,1152]{1,0:T(8,128)} %fusion.106, bf16[768,1152]{1,0:T(8,128)(2,1)} %bitcast.115, bf16[1152,1152]{1,0:T(8,128)(2,1)} %all-gather.7.cloned.1.call-done), kind=kOutput, calls=%fused_computation.202 | convolution fusion | flops 4093673472 | bytes 15040512 | tf_op jit(solution)/shard_map/dot_general | solution.py:89
  486.9 43.4 %reduce-scatter.5.cloned.1.call-done = f32[144,1152]{1,0:T(8,128)} async-done(((f32[1152,1152]{1,0:T(8,128)}), f32[144,1152]{1,0:T(8,128)}) %reduce-scatter.5.cloned.1.call-update) | async-done | bytes 663568 | tf_op jit(solution)/shard_map/reduce_scatter | solution.py:120
  530.3 60.9 %reduce-scatter.3.cloned.1.call-done = f32[144,1152]{1,0:T(8,128)} async-done(((f32[1152,1152]{1,0:T(8,128)}), f32[144,1152]{1,0:T(8,128)}) %reduce-scatter.3.cloned.1.call-update) | async-done | bytes 663568 | tf_op jit(solution)/shard_map/reduce_scatter | solution.py:120
  (159 shorter events, 59.2 us)
Async XLA Ops:
  7.2 14.0 %copy-start = (bf16[1000,1152]{1,0:T(8,128)(2,1)S(1)}, bf16[1000,1152]{1,0:T(8,128)(2,1)}, u32[]{:S(2)}) copy-start(bf16[1000,1152]{1,0:T(8,128)(2,1)} %param.19) | copy-start | bytes 6912004
  7.2 20.4 %copy-start.28 = (s32[3]{0:T(128)S(1)}, s32[3]{0:T(128)}, u32[]{:S(2)}) copy-start(s32[3]{0:T(128)} %param.17) | copy-start | bytes 40
  7.2 16.6 %copy-start.10 = (bf16[144,3,288]{2,0,1:T(8,128)(2,1)S(1)}, bf16[144,3,288]{2,0,1:T(8,128)(2,1)}, u32[]{:S(2)}) copy-start(bf16[144,3,288]{2,0,1:T(8,128)(2,1)} %param.26) | copy-start | bytes 746500
  7.2 21.1 %copy-start.29 = (s32[3]{0:T(128)S(1)}, s32[3]{0:T(128)}, u32[]{:S(2)}) copy-start(s32[3]{0:T(128)} %param.18) | copy-start | bytes 40
  7.2 21.1 %copy-start.19 = (f32[3,32,128]{2,1,0:T(8,128)S(1)}, f32[3,32,128]{2,1,0:T(8,128)}, u32[]{:S(2)}) copy-start(f32[3,32,128]{2,1,0:T(8,128)} %param.15) | copy-start | bytes 147460
  7.2 70.6 %all-reduce.13.cloned.1.call-start = ((), (), s32[]{:S(2)}) async-start(), calls=%async_computation.9 | async-start | bytes 663552
  24.9 186.8 %all-gather.11.cloned.1.call-start = ((), (), s32[]{:S(2)}) async-start(), calls=%async_computation.5 | async-start | bytes 2985984 | tf_op jit(solution)/shard_map/all_gather | solution.py:180
  25.6 186.1 %all-gather.9.cloned.1.call-start = ((), (), s32[]{:S(2)}) async-start(), calls=%async_computation.4 | async-start | bytes 2985984 | tf_op jit(solution)/shard_map/all_gather | solution.py:179
  26.4 198.6 %all-gather.5.cloned.1.call-start = ((), (), s32[]{:S(2)}) async-start(), calls=%async_computation.2 | async-start | bytes 2985984 | tf_op jit(solution)/shard_map/all_gather | solution.py:217
  27.0 204.7 %all-gather.7.cloned.1.call-start = ((), (), s32[]{:S(2)}) async-start(), calls=%async_computation.3 | async-start | bytes 2985984 | tf_op jit(solution)/shard_map/all_gather | solution.py:221
  27.5 266.3 %all-reduce.11.cloned.1.call-start = ((), (), s32[]{:S(2)}) async-start(), calls=%async_computation.6 | async-start | bytes 3538944 | tf_op jit(solution)/shard_map/psum | solution.py:109
  34.2 3.3 copy-start.4
  34.2 3.3 copy-start.7
  34.2 3.3 copy-start.20
  36.4 3.5 copy-start.21
  201.4 5.7 copy-start.23
  201.4 5.7 copy-start.24
  221.2 226.7 %all-reduce.15.cloned.1.call-start = ((), (), s32[]{:S(2)}) async-start(), calls=%async_computation.10 | async-start | bytes 7077888 | tf_op jit(solution)/shard_map/psum | solution.py:109
  300.1 2.6 copy-start.18
  314.9 215.4 %reduce-scatter.5.cloned.1.call-start = ((), (), s32[]{:S(2)}) async-start(), calls=%async_computation.8 | async-start | bytes 5971968 | tf_op jit(solution)/shard_map/reduce_scatter | solution.py:120
  462.0 4.7 copy-start.3
  462.0 4.7 copy-start.13
  474.3 116.9 %reduce-scatter.3.cloned.1.call-start = ((), (), s32[]{:S(2)}) async-start(), calls=%async_computation.7 | async-start | bytes 5971968 | tf_op jit(solution)/shard_map/reduce_scatter | solution.py:120
  474.6 116.6 %copy-start.1 = (bf16[1000,1152]{1,0:T(8,128)(2,1)S(1)}, bf16[1000,1152]{1,0:T(8,128)(2,1)}, u32[]{:S(2)}) copy-start(bf16[1000,1152]{1,0:T(8,128)(2,1)} %param.19) | copy-start | bytes 6912004
  (16 other events, 26.4 us)
Sparse Core Ops, SparseCore 0:
  25.0 52.8 all-reduce.12
  79.7 30.7 all-gather.10
  112.4 30.1 all-gather.8
  144.3 30.1 all-gather.4
  176.2 30.1 all-gather.6
  221.3 72.3 all-reduce.10
  315.0 132.8 all-reduce.14
  474.4 55.8 reduce-scatter.4
  534.3 56.8 reduce-scatter.2
where the time goes:
time: 607 us; the launch traced here: 598 us
  waiting for transfers between devices  326 us (54%)
  blocking collectives  110 us (18%)
  matrix products  66.2 us (11%)
  local copies, waits for them, and re-layouts  39.9 us (7%)
  other arithmetic  38.5 us (6%)
  between operations  16.2 us (3%)
    psum x2, waiting for transfers between devices, network(): mixed = lax.psum(partial_out, 'col').astype(jnp.float32)  186 us
    reduce_scatter x2, waiting for transfers between devices, reduce_gradient(): lax.psum_scatter(contract_first(left, right), ('dp', 'row'), scatter_dime...  104 us
    all_gather x1, blocking collectives, body(): lax.all_gather(teacher_sums, 'col', axis=3, tiled=True)  62.1 us
    all_gather x1, blocking collectives, body(): lax.all_gather(student_sums, 'col', axis=3, tiled=True)  38.8 us
    unnamed x10, waiting for transfers between devices  36.1 us
    dot_general x6, matrix products, contract_last(): lax.dot_general(left, right, (((1,), (1,)), ((), ())), preferred_element_...  29 us
    unnamed x77, local copies, waits for them, and re-layouts  21.6 us
    dot_general x2, matrix products, contract_first(): lax.dot_general(left, right, (((0,), (0,)), ((), ())), preferred_element_...  17.3 us
  transfers between devices with their start and end apart: 9, of which 5 were waited for; matrix products, arithmetic and copies ran while one was open for 15% of the time, Pallas kernels for 0%

commit v1 on v0

--- a/solution.py
+++ b/solution.py
@@ -106,7 +106,7 @@
     pre = up_product(act)
     hidden = jax.nn.gelu(pre, approximate=True).astype(jnp.bfloat16)
     partial_out = down_product(hidden).astype(jnp.bfloat16)
-    mixed = lax.psum(partial_out, "col").astype(jnp.float32)
+    mixed = jnp.sum(lax.all_gather(partial_out, "col"), axis=0).astype(jnp.float32)
     later = base + gate * mixed.reshape(samples, SEQ, D)
     final, reciprocal = layer_norm(later)
     velocity = contract_last(final.astype(jnp.bfloat16).reshape(samples * SEQ, D), out_weight)

time: 607 us -> 746 us (1.23)
  waiting for transfers between devices: 326 us -> 451 us
  other arithmetic: 38.5 us -> 55.4 us
    all_gather x0 -> x3, waiting for transfers between devices: none -> 304 us  [network(): lax.all_gather(partial_out, 'col')]
    psum x2 -> x0, waiting for transfers between devices: 186 us -> none  [network(): mixed = lax.psum(partial_out, 'col').astype(jnp.float32)]
    reduce_sum x0 -> x3, other arithmetic: none -> 17.3 us  [network(): jnp.sum(lax.all_gather(partial_out, 'col'), axis=0).astype(jnp.float32)]
    unnamed x10 -> x11, waiting for transfers between devices: 36.1 us -> 42.9 us
    unnamed x77 -> x71, local copies, waits for them, and re-layouts: 21.6 us -> 19.6 us
  transfers between devices with their start and end apart: 9 -> 10, of which waited for: 5 -> 6; matrix products, arithmetic and copies ran while one was open for 15% -> 17% of each run, Pallas kernels for 0% -> 0%
where the time goes in v1:
time: 746 us; the launch traced here: 739 us
  waiting for transfers between devices  451 us (60%)
  blocking collectives  110 us (15%)
  matrix products  67.6 us (9%)
  other arithmetic  55.4 us (7%)
  local copies, waits for them, and re-layouts  38.1 us (5%)
  between operations  16.5 us (2%)
    all_gather x3, waiting for transfers between devices, network(): lax.all_gather(partial_out, 'col')  304 us
    reduce_scatter x2, waiting for transfers between devices, reduce_gradient(): lax.psum_scatter(contract_first(left, right), ('dp', 'row'), scatter_dime...  103 us
    all_gather x1, blocking collectives, body(): lax.all_gather(teacher_sums, 'col', axis=3, tiled=True)  62.6 us
    unnamed x11, waiting for transfers between devices  42.9 us
    all_gather x1, blocking collectives, body(): lax.all_gather(student_sums, 'col', axis=3, tiled=True)  38.2 us
    dot_general x6, matrix products, contract_last(): lax.dot_general(left, right, (((1,), (1,)), ((), ())), preferred_element_...  28.8 us
    unnamed x71, local copies, waits for them, and re-layouts  19.6 us
    dot_general x2, matrix products, contract_first(): lax.dot_general(left, right, (((0,), (0,)), ((), ())), preferred_element_...  17.6 us
  transfers between devices with their start and end apart: 10, of which 6 were waited for; matrix products, arithmetic and copies ran while one was open for 17% of the time, Pallas kernels for 0%

profile of v1, /device:TPU:0, one launch (start us, length us, event | category | flops | bytes accessed | tf_op | source)
XLA Modules:
  0.0 739.3 jit_solution(6603615169965612273)
XLA Ops:
  11.1 9.5 %all-reduce.4 = (s32[24]{0:T(128)S(1)}, s32[24]{0:T(128)S(1)}) all-reduce(s32[24]{0:T(128)S(1)} %dynamic-update-slice, s32[24]{0:T(128)S(1)} %dynamic-update-slice.1), channel_id=1, replica_groups=mesh['dp'=2,'row'=4,'col'=4] {'dp','row'}, use_global_device_ids=true, to_apply=%add | all-reduce | flops 48 | bytes 384
  37.4 40.4 %all-reduce.8.cloned.1.call-done = (f32[24,1,3,288]{3,1,2,0:T(1,128)}, f32[24,2,3,288]{3,1,2,0:T(2,128)}) async-done(((f32[24,1,3,288]{3,1,2,0:T(1,128)}, f32[24,2,3,288]{3,1,2,0:T(2,128)}), (f32[24,1,3,288]{3,1,2,0:T(1,128)}, f32[24,2,3,288]{3,1,2,0:T(2,128)})) %all-reduce.8.cloned.1.call-update) | async-done | bytes 248848
  81.1 62.6 %all_gather.49 = f32[3,2,3,1152]{2,1,0,3:T(2,128)S(1)} all-gather(f32[3,2,3,288]{2,1,0,3:T(2,128)} %copy.57), channel_id=1, replica_groups=mesh['dp'=2,'row'=4,'col'=4] {'col'}, dimensions={3}, use_global_device_ids=true | all-gather | bytes 103680 | tf_op jit(solution)/shard_map/all_gather | solution.py:170
  143.8 3.9 fusion.98
  147.7 4.6 copy.81
  156.3 9.5 %convolution_convert_fusion.1 = bf16[768,1152]{1,0:T(8,128)(2,1)} fusion(bf16[1152,1152]{1,0:T(8,128)(2,1)} %all-gather.17.cloned.1.call-done, bf16[768,1152]{1,0:T(8,128)(2,1)} %bitcast.129, bf16[1152,1152]{1,0:T(8,128)(2,1)} %all-gather.15.cloned.1.call-done), kind=kOutput, calls=%fused_computation.59 | convolution fusion | flops 4085710848 | bytes 8847360 | tf_op jit(solution)/shard_map/dot_general | solution.py:83
  174.5 38.2 %all_gather.44 = f32[3,1,3,1152]{2,1,0,3:T(1,128)} all-gather(f32[3,1,3,288]{2,1,0,3:T(1,128)} %copy.52), channel_id=1, replica_groups=mesh['dp'=2,'row'=4,'col'=4] {'col'}, dimensions={3}, use_global_device_ids=true | all-gather | bytes 51840 | tf_op jit(solution)/shard_map/all_gather | solution.py:171
  212.8 4.6 copy.53
  219.0 4.7 add_convert_fusion.2
  223.7 6.7 fusion.110
  230.4 7.3 convolution_convert_fusion.2
  238.0 4.6 copy.82
  244.8 91.1 %all-gather.21.cloned.1.call-done = bf16[3072,1152]{1,0:T(8,128)(2,1)} async-done(((bf16[768,1152]{1,0:T(8,128)(2,1)}), bf16[3072,1152]{1,0:T(8,128)(2,1)}) %all-gather.21.cloned.1.call-update) | async-done | bytes 7077904 | tf_op jit(solution)/shard_map/all_gather | solution.py:109
  335.9 5.8 reduce_sum.169
  353.4 9.5 %convolution_convert_fusion = bf16[768,1152]{1,0:T(8,128)(2,1)} fusion(bf16[1152,1152]{1,0:T(8,128)(2,1)} %all-gather.17.cloned.1.call-done, bf16[768,1152]{1,0:T(8,128)(2,1)} %bitcast.130, bf16[1152,1152]{1,0:T(8,128)(2,1)} %all-gather.15.cloned.1.call-done), kind=kOutput, calls=%fused_computation.58 | convolution fusion | flops 4085710848 | bytes 8847360 | tf_op jit(solution)/shard_map/dot_general | solution.py:83
  363.9 100.0 %all-gather.19.cloned.1.call-done = bf16[3072,1152]{1,0:T(8,128)(2,1)} async-done(((bf16[768,1152]{1,0:T(8,128)(2,1)}), bf16[3072,1152]{1,0:T(8,128)(2,1)}) %all-gather.19.cloned.1.call-update) | async-done | bytes 7077904 | tf_op jit(solution)/shard_map/all_gather | solution.py:109
  463.9 5.8 reduce_sum.164
  478.7 113.2 %all-gather.23.cloned.1.call-done = bf16[3072,1152]{1,0:T(8,128)(2,1)} async-done(((bf16[768,1152]{1,0:T(8,128)(2,1)}), bf16[3072,1152]{1,0:T(8,128)(2,1)}) %all-gather.23.cloned.1.call-update) | async-done | bytes 7077904 | tf_op jit(solution)/shard_map/all_gather | solution.py:109
  591.8 5.8 reduce_sum.174
  603.3 4.6 fusion.93
  610.9 5.1 fusion.90
  616.1 12.5 %fusion.114 = f32[1152,1152]{1,0:T(8,128)} fusion(bf16[768,1152]{1,0:T(8,128)(2,1)} %bitcast.126, f32[768,1152]{1,0:T(8,128)} %fusion.110, bf16[768,1152]{1,0:T(8,128)(2,1)} %bitcast.128, bf16[1152,1152]{1,0:T(8,128)(2,1)} %all-gather.13.cloned.1.call-done), kind=kOutput, calls=%fused_computation.205 | convolution fusion | flops 4093673472 | bytes 15040512 | tf_op jit(solution)/shard_map/dot_general | solution.py:89
  628.6 42.6 %reduce-scatter.5.cloned.1.call-done = f32[144,1152]{1,0:T(8,128)} async-done(((f32[1152,1152]{1,0:T(8,128)}), f32[144,1152]{1,0:T(8,128)}) %reduce-scatter.5.cloned.1.call-update) | async-done | bytes 663568 | tf_op jit(solution)/shard_map/reduce_scatter | solution.py:120
  671.2 60.7 %reduce-scatter.3.cloned.1.call-done = f32[144,1152]{1,0:T(8,128)} async-done(((f32[1152,1152]{1,0:T(8,128)}), f32[144,1152]{1,0:T(8,128)}) %reduce-scatter.3.cloned.1.call-update) | async-done | bytes 663568 | tf_op jit(solution)/shard_map/reduce_scatter | solution.py:120
  (159 shorter events, 69.6 us)
Async XLA Ops:
  7.2 14.0 %copy-start = (bf16[1000,1152]{1,0:T(8,128)(2,1)S(1)}, bf16[1000,1152]{1,0:T(8,128)(2,1)}, u32[]{:S(2)}) copy-start(bf16[1000,1152]{1,0:T(8,128)(2,1)} %param.19) | copy-start | bytes 6912004
  7.2 20.4 %copy-start.25 = (s32[3]{0:T(128)S(1)}, s32[3]{0:T(128)}, u32[]{:S(2)}) copy-start(s32[3]{0:T(128)} %param.17) | copy-start | bytes 40
  7.2 16.6 %copy-start.8 = (bf16[144,3,288]{2,0,1:T(8,128)(2,1)S(1)}, bf16[144,3,288]{2,0,1:T(8,128)(2,1)}, u32[]{:S(2)}) copy-start(bf16[144,3,288]{2,0,1:T(8,128)(2,1)} %param.21) | copy-start | bytes 746500
  7.2 21.0 %copy-start.26 = (s32[3]{0:T(128)S(1)}, s32[3]{0:T(128)}, u32[]{:S(2)}) copy-start(s32[3]{0:T(128)} %param.18) | copy-start | bytes 40
  7.2 21.0 %copy-start.18 = (f32[3,32,128]{2,1,0:T(8,128)S(1)}, f32[3,32,128]{2,1,0:T(8,128)}, u32[]{:S(2)}) copy-start(f32[3,32,128]{2,1,0:T(8,128)} %param.15) | copy-start | bytes 147460
  7.2 70.6 %all-reduce.8.cloned.1.call-start = ((), (), s32[]{:S(2)}) async-start(), calls=%async_computation.11 | async-start | bytes 663552
  24.8 131.5 %all-gather.15.cloned.1.call-start = ((), (), s32[]{:S(2)}) async-start(), calls=%async_computation.4 | async-start | bytes 2985984 | tf_op jit(solution)/shard_map/all_gather | solution.py:179
  25.6 130.7 %all-gather.17.cloned.1.call-start = ((), (), s32[]{:S(2)}) async-start(), calls=%async_computation.5 | async-start | bytes 2985984 | tf_op jit(solution)/shard_map/all_gather | solution.py:180
  26.3 197.4 %all-gather.11.cloned.1.call-start = ((), (), s32[]{:S(2)}) async-start(), calls=%async_computation.2 | async-start | bytes 2985984 | tf_op jit(solution)/shard_map/all_gather | solution.py:217
  26.9 203.5 %all-gather.13.cloned.1.call-start = ((), (), s32[]{:S(2)}) async-start(), calls=%async_computation.3 | async-start | bytes 2985984 | tf_op jit(solution)/shard_map/all_gather | solution.py:221
  27.5 308.4 %all-gather.21.cloned.1.call-start = ((), (), s32[]{:S(2)}) async-start(), calls=%async_computation.9 | async-start | bytes 8847360 | tf_op jit(solution)/shard_map/all_gather | solution.py:109
  165.8 298.1 %all-gather.19.cloned.1.call-start = ((), (), s32[]{:S(2)}) async-start(), calls=%async_computation.8 | async-start | bytes 8847360 | tf_op jit(solution)/shard_map/all_gather | solution.py:109
  169.6 3.1 copy-start.19
  174.5 44.4 %copy-start.20 = (f32[3,256]{1,0:T(4,128)S(1)}, f32[3,256]{1,0:T(4,128)}, u32[]{:S(2)}) copy-start(f32[3,256]{1,0:T(4,128)} %copy-done.19) | copy-start | bytes 9220
  174.5 44.4 %copy-start.21 = (f32[3,256]{1,0:T(4,128)S(1)}, f32[3,256]{1,0:T(4,128)}, u32[]{:S(2)}) copy-start(f32[3,256]{1,0:T(4,128)} %add_rsqrt_fusion.5) | copy-start | bytes 9220
  237.7 4.9 copy-start.17
  237.7 354.1 %all-gather.23.cloned.1.call-start = ((), (), s32[]{:S(2)}) async-start(), calls=%async_computation.10 | async-start | bytes 8847360 | tf_op jit(solution)/shard_map/all_gather | solution.py:109
  348.2 2.6 copy-start.16
  363.0 308.3 %reduce-scatter.5.cloned.1.call-start = ((), (), s32[]{:S(2)}) async-start(), calls=%async_computation.7 | async-start | bytes 5971968 | tf_op jit(solution)/shard_map/reduce_scatter | solution.py:120
  603.3 4.7 copy-start.3
  603.3 4.7 copy-start.11
  608.0 2.9 copy-start.27
  616.0 116.0 %reduce-scatter.3.cloned.1.call-start = ((), (), s32[]{:S(2)}) async-start(), calls=%async_computation.6 | async-start | bytes 5971968 | tf_op jit(solution)/shard_map/reduce_scatter | solution.py:120
  616.1 115.9 %copy-start.1 = (bf16[1000,1152]{1,0:T(8,128)(2,1)S(1)}, bf16[1000,1152]{1,0:T(8,128)(2,1)}, u32[]{:S(2)}) copy-start(bf16[1000,1152]{1,0:T(8,128)(2,1)} %param.19) | copy-start | bytes 6912004
  (14 other events, 24.4 us)
Sparse Core Ops, SparseCore 0:
  25.0 52.7 all-reduce.7
  79.7 30.7 all-gather.14
  112.3 30.1 all-gather.16
  144.2 30.1 all-gather.10
  176.1 30.1 all-gather.12
  207.7 128.1 all-gather.20
  337.5 126.3 all-gather.18
  465.4 126.3 all-gather.22
  616.1 55.0 reduce-scatter.4
  675.1 56.8 reduce-scatter.2
